TPU v7x, 32 devices: a whole 2x2x4 slice. The times are simulated.
32 devices in a mesh: grp: 2 (over y), kvp: 4 (over z), tp: 4 (over x, core).
Axes of the slice: x: 2, y: 2, z: 4, core: 2. Of those that a mesh axis runs over, the one named last changes fastest.
Arguments:
- queries: bfloat16 [32, 4096], P('grp', 'tp'), parts along dimension 0, may hold values from -6 to 6
- keys: bfloat16 [32, 512, 512], P('grp', 'kvp', 'tp'), parts along dimension 0, may hold values from -6 to 6
- values: bfloat16 [32, 512, 512], P('grp', 'kvp', 'tp'), parts along dimension 0, may hold values from -6 to 6
- lengths: int32 [32], P('grp'), parts along dimension 0, may hold values from 256 to 512, as said below
- out_weight: bfloat16 [4096, 1536], P('tp', 'kvp'), may hold values from -0.375 to 0.375
- residual: bfloat16 [32, 1536], P('grp', 'kvp'), parts along dimension 0, may hold values from -20 to 20
- norm_gain: bfloat16 [1536], P('kvp'), may hold values from 0.099609375 to 1.8984375
- expert_ids: int32 [32, 4], P('grp'), parts along dimension 0, may hold values from 0 to 3, as said below
- gate_probs: float32 [32, 4], P('grp'), parts along dimension 0, may hold values from 0.2 to 1
- w_gate: bfloat16 [4, 1536, 1536], P('kvp', None, 'tp'), may hold values from -0.15625 to 0.15625
- w_up: bfloat16 [4, 1536, 1536], P('kvp', None, 'tp'), may hold values from -0.15625 to 0.15625
- w_down: bfloat16 [4, 1536, 1536], P('kvp', 'tp'), may hold values from -0.15625 to 0.15625
Outputs:
- attended: float32 [32, 4096], P('grp', 'tp'), parts along dimension 0
- mixed: bfloat16 [32, 1536], P('grp', 'kvp'), parts along dimension 0
There are 2 independent parts, one for each index of `grp`. A program takes and returns all parts, laid end to end along the dimension named above; an argument that names none is the same for every part. Nothing has to cross between parts.
Inputs may be any that keep to these rules, and one draw needn't show every extreme that they name: `lengths`: at least one sequence has all 512 positions valid. `expert_ids`: each row names 4 different experts; no expert is named by more than 16 rows, and some expert by exactly 16.
All inputs are finite; a program needn't handle non-finite values.
Results may differ from a plain program's by a relative error of at most 0.006.
Values may be sent and summed in bfloat16 or wider, within the bound.
No kernel may reach another device: no remote copies, remote signals or barrier semaphores. Data moves between devices by JAX's collectives and lax.ppermute only.
A program may use at most 64 MiB of HBM per device.

v0:
```python
import jax
import jax.numpy as jnp
from jax import lax
from jax.sharding import PartitionSpec as P

D = 1536
HEAD = 64
EPSILON = 1e-05
NEGATIVE = -1e30


def merged(part, axis, combine):
    gathered = jax.tree.map(lambda a: lax.all_gather(a, axis), part)

    def take(source):
        return jax.tree.map(lambda a: lax.dynamic_index_in_dim(a, source, 0, False), gathered)

    return lax.fori_loop(
        1, lax.axis_size(axis), lambda source, state: combine(state, take(source)), take(0)
    )


def slot_tables(expert_ids, gate_probs, experts, capacity):
    batch_size, top_count = expert_ids.shape
    flat_ids = expert_ids.reshape(-1)
    pair_count = flat_ids.shape[0]
    pair_order = jnp.arange(pair_count, dtype=jnp.int32)
    earlier_same = (flat_ids[:, None] == flat_ids[None, :]) & (
        pair_order[None, :] < pair_order[:, None]
    )
    slot_index = jnp.sum(earlier_same.astype(jnp.int32), axis=1)
    target_col = flat_ids * capacity + slot_index
    columns = jnp.arange(experts * capacity, dtype=jnp.int32)
    hit_table = (target_col[:, None] == columns[None, :]).astype(jnp.float32)
    hit_table = hit_table.reshape(batch_size, top_count, experts * capacity)
    dispatch = jnp.sum(hit_table, axis=1)
    combine = jnp.sum(hit_table * gate_probs[:, :, None], axis=1)
    return (dispatch, combine)


def merge_partial(earlier, latest):
    global_max = jnp.maximum(earlier[0], latest[0])
    lead_scale = jnp.exp(earlier[0] - global_max)
    trail_scale = jnp.exp(latest[0] - global_max)
    return (
        global_max,
        lead_scale * earlier[1] + trail_scale * latest[1],
        lead_scale[..., None] * earlier[2] + trail_scale[..., None] * latest[2],
    )


def on_device(
    queries,
    keys,
    values,
    lengths,
    out_weight,
    residual,
    norm_gain,
    expert_ids,
    gate_probs,
    w_gate,
    w_up,
    w_down,
):
    batch_size = queries.shape[0]
    local_kv = keys.shape[2] // HEAD
    local_heads = queries.shape[1] // HEAD
    group_size = local_heads // local_kv
    ctx_dev = keys.shape[1]
    shards = lax.axis_size("kvp")
    query_heads = queries.reshape(batch_size, local_kv, group_size, HEAD)
    key_rows = keys.reshape(batch_size, ctx_dev, local_kv, HEAD)
    value_rows = values.reshape(batch_size, ctx_dev, local_kv, HEAD)
    scores = jnp.einsum(
        "bgrd,bcgd->bgrc", query_heads, key_rows, preferred_element_type=jnp.float32
    ) * HEAD ** (-0.5)
    position = lax.axis_index("kvp") * ctx_dev + jnp.arange(ctx_dev, dtype=jnp.int32)
    valid_key = (position[None, :] < lengths[:, None])[:, None, None, :]
    masked = jnp.where(valid_key, scores, NEGATIVE)
    block_max = jnp.max(masked, axis=3)
    weights = jnp.where(valid_key, jnp.exp(masked - block_max[..., None]), 0.0)
    rounded = weights.astype(jnp.bfloat16)
    block_sum = jnp.sum(rounded.astype(jnp.float32), axis=3)
    block_out = jnp.einsum(
        "bgrc,bcgd->bgrd", rounded, value_rows, preferred_element_type=jnp.float32
    )
    global_max, denominator, summed = merged(
        (block_max, block_sum, block_out), "kvp", merge_partial
    )
    attended = (summed / denominator[..., None]).reshape(batch_size, local_heads * HEAD)
    projected = lax.psum(
        jnp.dot(attended.astype(jnp.bfloat16), out_weight, preferred_element_type=jnp.float32), "tp"
    )
    hidden_state = lax.optimization_barrier(
        (projected + residual.astype(jnp.float32)).astype(jnp.bfloat16)
    )
    state_wide = hidden_state.astype(jnp.float32)
    col_count = hidden_state.shape[1]
    exp_dev = w_gate.shape[0]
    experts = exp_dev * shards
    capacity = min(batch_size, max(2, 2 * batch_size * expert_ids.shape[1] // experts))
    dispatch, combine = slot_tables(expert_ids, gate_probs, experts, capacity)
    total_sq = lax.psum(jnp.sum(state_wide * state_wide, axis=1), "kvp")
    inverse = lax.rsqrt(total_sq / D + EPSILON)
    normed = (state_wide * inverse[:, None] * norm_gain.astype(jnp.float32)[None, :]).astype(
        jnp.bfloat16
    )
    outgoing = jnp.dot(
        dispatch.T.astype(jnp.bfloat16), normed, preferred_element_type=jnp.float32
    ).astype(jnp.bfloat16)
    outgoing = outgoing.reshape(experts, capacity, col_count)
    expert_rows = lax.all_to_all(outgoing, "kvp", split_axis=0, concat_axis=2, tiled=True)
    gate_proj = jnp.einsum("ecd,edf->ecf", expert_rows, w_gate, preferred_element_type=jnp.float32)
    up_proj = jnp.einsum("ecd,edf->ecf", expert_rows, w_up, preferred_element_type=jnp.float32)
    activation = (jax.nn.silu(gate_proj) * up_proj).astype(jnp.bfloat16)
    partial_value = jnp.einsum(
        "ecf,efd->ecd", activation, w_down, preferred_element_type=jnp.float32
    )
    returned = lax.all_to_all(partial_value, "kvp", split_axis=2, concat_axis=0, tiled=True)
    moe_local = jnp.dot(
        combine, returned.reshape(experts * capacity, col_count), precision=lax.Precision.HIGHEST
    )
    moe_term = lax.psum(moe_local, "tp")
    mixed = (state_wide + moe_term).astype(jnp.bfloat16)
    return (attended, mixed)


def solution(mesh):
    return jax.shard_map(
        on_device,
        mesh=mesh,
        in_specs=(
            P("grp", "tp"),
            P("grp", "kvp", "tp"),
            P("grp", "kvp", "tp"),
            P("grp"),
            P("tp", "kvp"),
            P("grp", "kvp"),
            P("kvp"),
            P("grp", None),
            P("grp", None),
            P("kvp", None, "tp"),
            P("kvp", None, "tp"),
            P("kvp", "tp", None),
        ),
        out_specs=(P("grp", "tp"), P("grp", "kvp")),
        check_vma=False,
    )
```

profile of v0, /device:TPU:0, one launch (start us, length us, event | category | flops | bytes accessed | tf_op | source)
XLA Modules:
  0.0 124.9 jit_solution(10427162739778779653)
XLA Ops:
  0.7 0.8 convert_element_type.54
  1.4 0.8 copy.99
  2.6 1.3 %multiply_add_fusion = s32[16,4]{0,1:T(4,128)} fusion(s32[16,4]{0,1:T(4,128)S(1)} %copy.100, s32[16,4]{0,1:T(4,128)} %param.21), kind=kLoop, calls=%fused_computation.48 | loop fusion | flops 128 | bytes 768 | tf_op jit(solution)/shard_map/add | solution.py:32
  3.9 0.9 reshape.104
  4.8 1.4 %copy.90 = bf16[16,128,128]{1,2,0:T(8,128)(2,1)S(1)} copy(bf16[16,128,128]{2,1,0:T(8,128)(2,1)} %param.15) | data formatting | bytes 1048576 | tf_op args[1]
  6.6 14.9 %all-gather = f32[64,2,8]{2,1,0:T(2,128)S(1)} all-gather(f32[16,2,8]{2,1,0:T(2,128)S(1)} %get-tuple-element.236), channel_id=2, replica_groups=mesh['grp'=2,'kvp'=4,'tp'=4] {'kvp'}, dimensions={0}, use_global_device_ids=true | all-gather | bytes 5120 | tf_op jit(solution)/shard_map/all_gather | solution.py:13
  21.7 13.3 %all-gather.1 = f32[64,2,8]{2,1,0:T(2,128)S(1)} all-gather(f32[16,2,8]{2,1,0:T(2,128)S(1)} %convert_reduce_fusion), channel_id=3, replica_groups=mesh['grp'=2,'kvp'=4,'tp'=4] {'kvp'}, dimensions={0}, use_global_device_ids=true | all-gather | bytes 5120 | tf_op jit(solution)/shard_map/all_gather | solution.py:13
  36.1 15.1 %all-gather.2 = f32[64,2,8,64]{3,2,1,0:T(8,128)S(1)} all-gather(f32[16,2,8,64]{3,2,1,0:T(8,128)S(1)} %fusion.35), channel_id=4, replica_groups=mesh['grp'=2,'kvp'=4,'tp'=4] {'kvp'}, dimensions={0}, use_global_device_ids=true | all-gather | bytes 327680 | tf_op jit(solution)/shard_map/all_gather | solution.py:13
  51.3 1.1 while.19
  52.6 0.7 reshape.107
  53.4 2.1 %fusion.18 = f32[16,384]{1,0:T(8,128)} fusion(bf16[1024,384]{1,0:T(8,128)(2,1)} %param.18, f32[16,1024]{1,0:T(8,128)} %reshape.107), kind=kOutput, calls=%fused_computation.30 | convolution fusion | flops 12599296 | bytes 876544 | tf_op jit(solution)/shard_map/dot_general | solution.py:93
  55.4 11.4 %psum.21 = f32[16,384]{1,0:T(8,128)} all-reduce(f32[16,384]{1,0:T(8,128)} %fusion.18), channel_id=1, replica_groups=mesh['grp'=2,'kvp'=4,'tp'=4] {'tp'}, use_global_device_ids=true, to_apply=%region_4.5 | all-reduce | flops 6144 | bytes 49152 | tf_op jit(solution)/shard_map/psum | solution.py:92
  66.8 0.7 add_convert_fusion
  68.2 12.5 %psum.22 = f32[16]{0:T(128)} all-reduce(f32[16]{0:T(128)} %fusion.21), channel_id=1, replica_groups=mesh['grp'=2,'kvp'=4,'tp'=4] {'kvp'}, use_global_device_ids=true, to_apply=%region_9.10 | all-reduce | flops 16 | bytes 128 | tf_op jit(solution)/shard_map/psum | solution.py:104
  80.7 0.7 add_rsqrt_fusion
  81.4 1.4 %convert_reduce_fusion.1 = (bf16[16,64]{1,0:T(8,128)(2,1)S(1)}, f32[16,64]{1,0:T(8,128)}) fusion(s32[16,4]{0,1:T(4,128)} %multiply_add_fusion, f32[16,4]{0,1:T(4,128)} %param.22), kind=kLoop, calls=%fused_computation.25 | loop fusion | flops 18432 | bytes 6656 | tf_op jit(solution)/shard_map/reduce_sum | solution.py:36
  82.9 8.1 %all_to_all.30 = bf16[4,16,384]{2,1,0:T(8,128)(2,1)S(1)} all-to-all(bf16[4,16,384]{2,1,0:T(8,128)(2,1)S(1)} %bitcast.73), channel_id=1, replica_groups=mesh['grp'=2,'kvp'=4,'tp'=4] {'kvp'}, dimensions={0} | all-to-all | bytes 98304 | tf_op jit(solution)/shard_map/all_to_all | solution.py:113
  91.6 1.7 %fusion.7 = f32[16,384]{1,0:T(8,128)} fusion(bf16[16,1536]{1,0:T(8,128)(2,1)} %bitcast.23, bf16[1,1536,384]{2,1,0:T(8,128)(2,1)S(1)} %copy-done.2), kind=kOutput, calls=%fused_computation.12 | convolution fusion | flops 18874368 | bytes 1253376 | tf_op jit(solution)/shard_map/ecd,edf->ecf/dot_general | solution.py:114
  93.3 1.6 %fusion.3 = f32[16,1536]{0,1:T(8,128)S(1)} fusion(bf16[1,384,1536]{2,1,0:T(8,128)(2,1)S(1)} %copy-done, bf16[16,1536]{1,0:T(8,128)(2,1)} %bitcast.23, bf16[1,1536,384]{2,1,0:T(8,128)(2,1)S(1)} %copy-done.1, f32[16,384]{1,0:T(8,128)} %fusion.7), kind=kOutput, calls=%fused_computation.8 | convolution fusion | flops 37785600 | bytes 2531328 | tf_op jit(solution)/shard_map/ecf,efd->ecd/dot_general | solution.py:117
  95.6 7.2 %reduce = f32[1536,16]{1,0:T(8,128)S(1)} reduce(f32[1536,1,16]{2,1,0:T(1,128)S(1)} %bitcast.66, f32[]{:T(128)} %broadcast.55), dimensions={1}, to_apply=%bitcast.47.reduce_sub_computation | reduce | bytes 196612
  103.1 8.2 %all_to_all.31 = f32[4,1,6144]{2,1,0:T(1,128)S(1)} all-to-all(f32[4,1,6144]{2,1,0:T(1,128)S(1)} %reshape.123), channel_id=1, replica_groups=mesh['grp'=2,'kvp'=4,'tp'=4] {'kvp'}, dimensions={0} | all-to-all | bytes 196608 | tf_op jit(solution)/shard_map/all_to_all | solution.py:120
  111.3 0.9 reduce.1
  112.3 1.3 %reshape.124 = f32[1536,1,16]{2,1,0:T(1,128)S(1)} reshape(f32[4,6144]{1,0:T(4,128)S(1)} %reduce.1) | data formatting | bytes 196608
  114.0 10.3 %psum.23 = f32[16,384]{1,0:T(8,128)S(1)} all-reduce(f32[16,384]{1,0:T(8,128)S(1)} %fusion.40), channel_id=1, replica_groups=mesh['grp'=2,'kvp'=4,'tp'=4] {'tp'}, use_global_device_ids=true, to_apply=%region_10.11 | all-reduce | flops 6144 | bytes 49152 | tf_op jit(solution)/shard_map/psum | solution.py:124
  (53 shorter events, 6.8 us)
Async XLA Ops:
  0.6 92.7 %copy-start = (bf16[1,384,1536]{2,1,0:T(8,128)(2,1)S(1)}, bf16[1,384,1536]{2,1,0:T(8,128)(2,1)}, u32[]{:S(2)}) copy-start(bf16[1,384,1536]{2,1,0:T(8,128)(2,1)} %param.25) | copy-start | bytes 3538948
  0.6 5.5 %copy-start.5 = (s32[16]{0:T(128)S(1)}, s32[16]{0:T(128)}, u32[]{:S(2)}) copy-start(s32[16]{0:T(128)} %param.17) | copy-start | bytes 196
  4.8 30.6 %copy-start.3 = (bf16[16,128,128]{2,1,0:T(8,128)(2,1)S(1)}, bf16[16,128,128]{2,1,0:T(8,128)(2,1)}, u32[]{:S(2)}) copy-start(bf16[16,128,128]{2,1,0:T(8,128)(2,1)} %param.16) | copy-start | bytes 1572868
  52.4 39.2 %copy-start.2 = (bf16[1,1536,384]{2,1,0:T(8,128)(2,1)S(1)}, bf16[1,1536,384]{2,1,0:T(8,128)(2,1)}, u32[]{:S(2)}) copy-start(bf16[1,1536,384]{2,1,0:T(8,128)(2,1)} %param.23) | copy-start | bytes 3538948
  53.4 40.0 %copy-start.1 = (bf16[1,1536,384]{2,1,0:T(8,128)(2,1)S(1)}, bf16[1,1536,384]{2,1,0:T(8,128)(2,1)}, u32[]{:S(2)}) copy-start(bf16[1,1536,384]{2,1,0:T(8,128)(2,1)} %param.24) | copy-start | bytes 3538948
  103.1 10.8 %copy-start.4 = (f32[16,64]{1,0:T(8,128)S(1)}, f32[16,64]{1,0:T(8,128)}, u32[]{:S(2)}) copy-start(f32[16,64]{1,0:T(8,128)} %get-tuple-element.217) | copy-start | bytes 12292
where the time goes:
time: 126 us; the launch traced here: 125 us
  blocking collectives  93.8 us (74%)
  other arithmetic  15.3 us (12%)
  local copies, waits for them, and re-layouts  8.31 us (7%)
  matrix products  6.53 us (5%)
    all_gather x3, blocking collectives, merged(): gathered = jax.tree.map(lambda a: lax.all_gather(a, axis), part)  43.4 us
    psum x1, blocking collectives, on_device(): total_sq = lax.psum(jnp.sum(state_wide * state_wide, axis=1), 'kvp')  12.5 us
    psum x1, blocking collectives, on_device(): lax.psum(jnp.dot(attended.astype(jnp.bfloat16), out_weight, preferred_ele...  11.4 us
    psum x1, blocking collectives, on_device(): moe_term = lax.psum(moe_local, 'tp')  10.3 us
    all_to_all x1, blocking collectives, on_device(): lax.all_to_all(partial_value, 'kvp', split_axis=2, concat_axis=0, tiled=T...  8.21 us
    all_to_all x1, blocking collectives, on_device(): lax.all_to_all(outgoing, 'kvp', split_axis=0, concat_axis=2, tiled=True)  8.06 us
    unnamed x1, other arithmetic  7.21 us
    unnamed x19, local copies, waits for them, and re-layouts  5.3 us

commit v1 on v0

--- a/solution.py
+++ b/solution.py
@@ -121,7 +121,9 @@
     moe_local = jnp.dot(
         combine, returned.reshape(experts * capacity, col_count), precision=lax.Precision.HIGHEST
     )
-    moe_term = lax.psum(moe_local, "tp")
+    moe_term = moe_local
+    for hop in (1, 2):
+        moe_term = moe_term + lax.ppermute(moe_term, "tp", [(dev, dev ^ hop) for dev in range(4)])
     mixed = (state_wide + moe_term).astype(jnp.bfloat16)
     return (attended, mixed)
 

time: 126 us -> 120 us (0.952)
  blocking collectives: 93.8 us -> 83.5 us
  waiting for transfers between devices: 0 us -> 3.26 us
  starting transfers between devices: 0 us -> 1.81 us
    psum x1 -> x0, blocking collectives: 10.3 us -> none  [on_device(): moe_term = lax.psum(moe_local, 'tp')]
    ppermute x0 -> x2, waiting for transfers between devices: none -> 3.26 us  [on_device(): lax.ppermute(moe_term, 'tp', [(dev, dev ^ hop) for dev in range(4)])]
    ppermute x0 -> x2, starting transfers between devices: none -> 1.81 us  [on_device(): lax.ppermute(moe_term, 'tp', [(dev, dev ^ hop) for dev in range(4)])]
  transfers between devices with their start and end apart: 0 -> 2, of which waited for: 0 -> 2; matrix products, arithmetic and copies ran while one was open for 0% -> 0% of each run, Pallas kernels for 0% -> 0%
where the time goes in v1:
time: 120 us
  blocking collectives  83.5 us (70%)
  other arithmetic  15.4 us (13%)
  local copies, waits for them, and re-layouts  8.31 us (7%)
  matrix products  6.53 us (5%)
  waiting for transfers between devices  3.26 us (3%)
  starting transfers between devices  1.81 us (2%)
    all_gather x3, blocking collectives, merged(): gathered = jax.tree.map(lambda a: lax.all_gather(a, axis), part)  43.4 us
    psum x1, blocking collectives, on_device(): total_sq = lax.psum(jnp.sum(state_wide * state_wide, axis=1), 'kvp')  12.5 us
    psum x1, blocking collectives, on_device(): lax.psum(jnp.dot(attended.astype(jnp.bfloat16), out_weight, preferred_ele...  11.4 us
    all_to_all x1, blocking collectives, on_device(): lax.all_to_all(partial_value, 'kvp', split_axis=2, concat_axis=0, tiled=T...  8.21 us
    all_to_all x1, blocking collectives, on_device(): lax.all_to_all(outgoing, 'kvp', split_axis=0, concat_axis=2, tiled=True)  8.06 us
    unnamed x1, other arithmetic  7.21 us
    unnamed x19, local copies, waits for them, and re-layouts  5.3 us
    ppermute x2, waiting for transfers between devices, on_device(): lax.ppermute(moe_term, 'tp', [(dev, dev ^ hop) for dev in range(4)])  3.26 us
  transfers between devices with their start and end apart: 2, of which 2 were waited for; matrix products, arithmetic and copies ran while one was open for 0% of the time, Pallas kernels for 0%

profile of v1, /device:TPU:0, one launch (start us, length us, event | category | flops | bytes accessed | tf_op | source)
XLA Modules:
  0.0 119.7 jit_solution(7369977174813172955)
XLA Ops:
  0.7 0.8 convert_element_type.54
  1.4 0.8 copy.99
  2.6 1.3 %multiply_add_fusion = s32[16,4]{0,1:T(4,128)} fusion(s32[16,4]{0,1:T(4,128)S(1)} %copy.100, s32[16,4]{0,1:T(4,128)} %param.21), kind=kLoop, calls=%fused_computation.48 | loop fusion | flops 128 | bytes 768 | tf_op jit(solution)/shard_map/add | solution.py:32
  3.9 0.9 reshape.104
  4.8 1.4 %copy.90 = bf16[16,128,128]{1,2,0:T(8,128)(2,1)S(1)} copy(bf16[16,128,128]{2,1,0:T(8,128)(2,1)} %param.15) | data formatting | bytes 1048576 | tf_op args[1]
  6.6 14.9 %all-gather = f32[64,2,8]{2,1,0:T(2,128)S(1)} all-gather(f32[16,2,8]{2,1,0:T(2,128)S(1)} %get-tuple-element.236), channel_id=2, replica_groups=mesh['grp'=2,'kvp'=4,'tp'=4] {'kvp'}, dimensions={0}, use_global_device_ids=true | all-gather | bytes 5120 | tf_op jit(solution)/shard_map/all_gather | solution.py:13
  21.7 13.3 %all-gather.1 = f32[64,2,8]{2,1,0:T(2,128)S(1)} all-gather(f32[16,2,8]{2,1,0:T(2,128)S(1)} %convert_reduce_fusion), channel_id=3, replica_groups=mesh['grp'=2,'kvp'=4,'tp'=4] {'kvp'}, dimensions={0}, use_global_device_ids=true | all-gather | bytes 5120 | tf_op jit(solution)/shard_map/all_gather | solution.py:13
  36.1 15.1 %all-gather.2 = f32[64,2,8,64]{3,2,1,0:T(8,128)S(1)} all-gather(f32[16,2,8,64]{3,2,1,0:T(8,128)S(1)} %fusion.35), channel_id=4, replica_groups=mesh['grp'=2,'kvp'=4,'tp'=4] {'kvp'}, dimensions={0}, use_global_device_ids=true | all-gather | bytes 327680 | tf_op jit(solution)/shard_map/all_gather | solution.py:13
  51.3 1.1 while.19
  53.4 2.1 %fusion.18 = f32[16,384]{1,0:T(8,128)} fusion(bf16[1024,384]{1,0:T(8,128)(2,1)} %param.18, f32[16,1024]{1,0:T(8,128)} %reshape.107), kind=kOutput, calls=%fused_computation.30 | convolution fusion | flops 12599296 | bytes 876544 | tf_op jit(solution)/shard_map/dot_general | solution.py:93
  55.4 11.4 %psum.14 = f32[16,384]{1,0:T(8,128)} all-reduce(f32[16,384]{1,0:T(8,128)} %fusion.18), channel_id=1, replica_groups=mesh['grp'=2,'kvp'=4,'tp'=4] {'tp'}, use_global_device_ids=true, to_apply=%region_4.5 | all-reduce | flops 6144 | bytes 49152 | tf_op jit(solution)/shard_map/psum | solution.py:92
  66.8 0.7 add_convert_fusion
  68.2 12.5 %psum.15 = f32[16]{0:T(128)} all-reduce(f32[16]{0:T(128)} %fusion.21), channel_id=1, replica_groups=mesh['grp'=2,'kvp'=4,'tp'=4] {'kvp'}, use_global_device_ids=true, to_apply=%region_9.10 | all-reduce | flops 16 | bytes 128 | tf_op jit(solution)/shard_map/psum | solution.py:104
  81.4 1.4 %convert_reduce_fusion.1 = (bf16[16,64]{1,0:T(8,128)(2,1)S(1)}, f32[16,64]{1,0:T(8,128)}) fusion(s32[16,4]{0,1:T(4,128)} %multiply_add_fusion, f32[16,4]{0,1:T(4,128)} %param.22), kind=kLoop, calls=%fused_computation.25 | loop fusion | flops 18432 | bytes 6656 | tf_op jit(solution)/shard_map/reduce_sum | solution.py:36
  82.9 8.1 %all_to_all.30 = bf16[4,16,384]{2,1,0:T(8,128)(2,1)S(1)} all-to-all(bf16[4,16,384]{2,1,0:T(8,128)(2,1)S(1)} %bitcast.73), channel_id=1, replica_groups=mesh['grp'=2,'kvp'=4,'tp'=4] {'kvp'}, dimensions={0} | all-to-all | bytes 98304 | tf_op jit(solution)/shard_map/all_to_all | solution.py:113
  91.6 1.7 %fusion.7 = f32[16,384]{1,0:T(8,128)} fusion(bf16[16,1536]{1,0:T(8,128)(2,1)} %bitcast.23, bf16[1,1536,384]{2,1,0:T(8,128)(2,1)S(1)} %copy-done.2), kind=kOutput, calls=%fused_computation.12 | convolution fusion | flops 18874368 | bytes 1253376 | tf_op jit(solution)/shard_map/ecd,edf->ecf/dot_general | solution.py:114
  93.3 1.6 %fusion.3 = f32[16,1536]{0,1:T(8,128)S(1)} fusion(bf16[1,384,1536]{2,1,0:T(8,128)(2,1)S(1)} %copy-done, bf16[16,1536]{1,0:T(8,128)(2,1)} %bitcast.23, bf16[1,1536,384]{2,1,0:T(8,128)(2,1)S(1)} %copy-done.1, f32[16,384]{1,0:T(8,128)} %fusion.7), kind=kOutput, calls=%fused_computation.8 | convolution fusion | flops 37785600 | bytes 2531328 | tf_op jit(solution)/shard_map/ecf,efd->ecd/dot_general | solution.py:117
  95.6 7.2 %reduce = f32[1536,16]{1,0:T(8,128)S(1)} reduce(f32[1536,1,16]{2,1,0:T(1,128)S(1)} %bitcast.66, f32[]{:T(128)} %broadcast.55), dimensions={1}, to_apply=%bitcast.47.reduce_sub_computation | reduce | bytes 196612
  103.1 8.2 %all_to_all.31 = f32[4,1,6144]{2,1,0:T(1,128)S(1)} all-to-all(f32[4,1,6144]{2,1,0:T(1,128)S(1)} %reshape.123), channel_id=1, replica_groups=mesh['grp'=2,'kvp'=4,'tp'=4] {'kvp'}, dimensions={0} | all-to-all | bytes 196608 | tf_op jit(solution)/shard_map/all_to_all | solution.py:120
  111.3 0.9 reduce.1
  112.3 1.3 %reshape.124 = f32[1536,1,16]{2,1,0:T(1,128)S(1)} reshape(f32[4,6144]{1,0:T(4,128)S(1)} %reduce.1) | data formatting | bytes 196608
  114.1 1.2 collective-permute-done
  115.3 1.7 %collective-permute-start.1 = (f32[16,384]{1,0:T(8,128)S(1)}, f32[16,384]{1,0:T(8,128)S(1)}, u32[]{:S(2)}, u32[]{:S(2)}) collective-permute-start(f32[16,384]{1,0:T(8,128)S(1)} %add.107), channel_id=1, source_target_pairs={{0,2},{1,3},{2,0},{3,1},{4,6},{5,7},{6,4},{7,5},{8,10},{9,11},{10,... | collective-permute-start | bytes 73736 | tf_op jit(solution)/shard_map/ppermute | solution.py:126
  117.0 2.1 %collective-permute-done.1 = f32[16,384]{1,0:T(8,128)S(1)} collective-permute-done((f32[16,384]{1,0:T(8,128)S(1)}, f32[16,384]{1,0:T(8,128)S(1)}, u32[]{:S(2)}, u32[]{:S(2)}) %collective-permute-start.1) | collective-permute-done | bytes 24608 | tf_op jit(solution)/shard_map/ppermute | solution.py:126
  (57 shorter events, 8.3 us)
Async XLA Ops:
  0.6 92.7 %copy-start = (bf16[1,384,1536]{2,1,0:T(8,128)(2,1)S(1)}, bf16[1,384,1536]{2,1,0:T(8,128)(2,1)}, u32[]{:S(2)}) copy-start(bf16[1,384,1536]{2,1,0:T(8,128)(2,1)} %param.25) | copy-start | bytes 3538948
  0.6 5.5 %copy-start.5 = (s32[16]{0:T(128)S(1)}, s32[16]{0:T(128)}, u32[]{:S(2)}) copy-start(s32[16]{0:T(128)} %param.17) | copy-start | bytes 196
  4.8 30.6 %copy-start.3 = (bf16[16,128,128]{2,1,0:T(8,128)(2,1)S(1)}, bf16[16,128,128]{2,1,0:T(8,128)(2,1)}, u32[]{:S(2)}) copy-start(bf16[16,128,128]{2,1,0:T(8,128)(2,1)} %param.16) | copy-start | bytes 1572868
  52.4 39.2 %copy-start.2 = (bf16[1,1536,384]{2,1,0:T(8,128)(2,1)S(1)}, bf16[1,1536,384]{2,1,0:T(8,128)(2,1)}, u32[]{:S(2)}) copy-start(bf16[1,1536,384]{2,1,0:T(8,128)(2,1)} %param.23) | copy-start | bytes 3538948
  53.4 40.0 %copy-start.1 = (bf16[1,1536,384]{2,1,0:T(8,128)(2,1)S(1)}, bf16[1,1536,384]{2,1,0:T(8,128)(2,1)}, u32[]{:S(2)}) copy-start(bf16[1,1536,384]{2,1,0:T(8,128)(2,1)} %param.24) | copy-start | bytes 3538948
  103.1 10.8 %copy-start.4 = (f32[16,64]{1,0:T(8,128)S(1)}, f32[16,64]{1,0:T(8,128)}, u32[]{:S(2)}) copy-start(f32[16,64]{1,0:T(8,128)} %get-tuple-element.217) | copy-start | bytes 12292
  114.0 1.3 %collective-permute-start = (f32[16,384]{1,0:T(8,128)S(1)}, f32[16,384]{1,0:T(8,128)S(1)}, u32[]{:S(2)}, u32[]{:S(2)}) collective-permute-start(f32[16,384]{1,0:T(8,128)S(1)} %fusion.40), channel_id=1, source_target_pairs={{0,1},{1,0},{2,3},{3,2},{4,5},{5,4},{6,7},{7,6},{8,9},{9,8},{10,11... | collective-permute-start | bytes 73736 | tf_op jit(solution)/shard_map/ppermute | solution.py:126
  115.3 3.8 %collective-permute-start.1 = (f32[16,384]{1,0:T(8,128)S(1)}, f32[16,384]{1,0:T(8,128)S(1)}, u32[]{:S(2)}, u32[]{:S(2)}) collective-permute-start(f32[16,384]{1,0:T(8,128)S(1)} %add.107), channel_id=1, source_target_pairs={{0,2},{1,3},{2,0},{3,1},{4,6},{5,7},{6,4},{7,5},{8,10},{9,11},{10,... | collective-permute-start | bytes 73736 | tf_op jit(solution)/shard_map/ppermute | solution.py:126
